TPU v7x, 32 devices: a whole 2x2x4 slice. The times are simulated.
32 devices in a mesh: channel: 4 (over z), tm: 4 (over y, core), beam: 2 (over x).
Axes of the slice: x: 2, y: 2, z: 4, core: 2. Of those that a mesh axis runs over, the one named last changes fastest.
Arguments:
- voltages: bfloat16 [2, 2048, 64, 1024], P(None, ('beam', 'channel'), None, 'tm'), may hold values from -6 to 6
- positions: int32 [2048], replicated, may hold values from 0 to 1023
- delays: int32 [32, 1024], P(None, 'channel'), may hold values from 0 to 63
Outputs:
- intensity: float32 [1024, 64, 1024], P(('beam', 'tm'), 'channel')
- dedispersed: float32 [1024, 32, 64], P(('beam', 'tm'), 'channel')
Inputs may be any that keep to these rules, and one draw needn't show every extreme that they name: `positions`: place on a grid of 4 cylinders by 256 places along each.
All inputs are finite; a program needn't handle non-finite values.
Results may differ from a plain program's by a relative error of at most 0.0071.
Values may be sent and summed in bfloat16 or wider, within the bound.
No kernel may reach another device: no remote copies, remote signals or barrier semaphores. Data moves between devices by JAX's collectives and lax.ppermute only.
A program may use at most 192 MiB of HBM per device.

v0:
```python
import math
import jax
import jax.numpy as jnp
from jax import lax
from jax.sharding import PartitionSpec as P

FEEDS = 2048
BEAMS = 1024
UPCH = 16
TAPS = 8
FINE = 1024
TWO_PI = 2.0 * math.pi
HIGHEST = lax.Precision.HIGHEST


def from_behind(value, axis, steps):
    count = lax.axis_size(axis)
    first, last = (max(0, -steps), min(count, count - steps))
    return lax.ppermute(value, axis, [(source, source + steps) for source in range(first, last)])


def window_table(tap_count, upch_factor):
    length = tap_count * upch_factor
    sample_index = jnp.arange(length).astype(jnp.float32)
    taper = jnp.sinc((sample_index - (length - 1) / 2.0) / upch_factor) * (
        0.5 - 0.5 * jnp.cos(TWO_PI * (sample_index + 0.5) / length)
    )
    taper = taper / jnp.sqrt(jnp.sum(taper * taper))
    return taper.reshape(tap_count, upch_factor)


def steering(positions, beam_start, item_count, places, feed_count):
    beam_ids = beam_start + jnp.arange(item_count)
    beam_east = beam_ids // places
    beam_north = beam_ids % places
    cylinder = positions // places
    along_row = positions % places
    coarse = beam_east[:, None] * cylinder[None, :] % 4
    north_turns = beam_north[:, None] * along_row[None, :] % places
    angles = TWO_PI * (coarse.astype(jnp.float32) / 4.0 + north_turns.astype(jnp.float32) / places)
    norm_scale = 1.0 / math.sqrt(feed_count)
    w_real = (jnp.cos(angles) * norm_scale).astype(jnp.bfloat16)
    w_imag = (-jnp.sin(angles) * norm_scale).astype(jnp.bfloat16)
    top_half = jnp.concatenate([w_real, -w_imag], axis=1)
    low_half = jnp.concatenate([w_imag, w_real], axis=1)
    return jnp.concatenate([top_half, low_half], axis=0)


def upchannel_matrix(upch_factor):
    sample_index = jnp.arange(128)
    frame_part = sample_index // upch_factor
    inner = sample_index % upch_factor
    same_frame = frame_part[:, None] == frame_part[None, :]
    angles = (inner[:, None] * inner[None, :] % upch_factor).astype(jnp.float32) * (
        TWO_PI / upch_factor
    )
    cos_part = jnp.where(same_frame, jnp.cos(angles), 0.0)
    sin_part = jnp.where(same_frame, -jnp.sin(angles), 0.0)
    top_half = jnp.concatenate([cos_part, sin_part], axis=1)
    low_half = jnp.concatenate([-sin_part, cos_part], axis=1)
    return jnp.concatenate([top_half, low_half], axis=0)


def per_device(voltages, positions, delays):
    places = BEAMS // 4
    by_channel = lax.all_to_all(voltages, "channel", split_axis=2, concat_axis=1, tiled=True)
    chan_count = by_channel.shape[2]
    sample_count = by_channel.shape[3]
    own_beams = BEAMS // lax.axis_size("beam")
    beam_start = lax.axis_index("beam") * own_beams
    feed_piece = lax.all_gather(by_channel, "beam", axis=1, tiled=True)
    piece_width = feed_piece.shape[1]
    weights = steering(positions, beam_start, own_beams, places, FEEDS)
    flat_piece = feed_piece.reshape(2 * piece_width, chan_count * sample_count)
    summed = jnp.dot(weights, flat_piece, preferred_element_type=jnp.float32)
    beams = summed.astype(jnp.bfloat16).reshape(2, own_beams, chan_count, sample_count)
    beam_count = beams.shape[1]
    chan_count = beams.shape[2]
    sample_count = beams.shape[3]
    rim_width = (TAPS - 1) * UPCH
    previous = from_behind(beams[:, :, :, sample_count - rim_width :], "tm", 1)
    extended = jnp.concatenate([previous, beams], axis=3)
    window = window_table(TAPS, UPCH)
    filtered = jnp.zeros(beams.shape, jnp.float32)
    for tap_index in range(TAPS):
        filtered = filtered + extended[
            :, :, :, tap_index * UPCH : tap_index * UPCH + sample_count
        ] * jnp.tile(window[tap_index], sample_count // UPCH)
    row_count = beam_count * chan_count
    tile_count = sample_count // 128
    halves = filtered.reshape(2, row_count, tile_count, 128)
    paired = jnp.concatenate([halves[0], halves[1]], axis=2)
    spectra = jnp.dot(paired, upchannel_matrix(UPCH), precision=HIGHEST)
    real_part = spectra[:, :, :128]
    imag_part = spectra[:, :, 128:]
    power_grid = (real_part * real_part + imag_part * imag_part).reshape(
        beam_count, chan_count, sample_count
    )
    intensity = lax.all_to_all(power_grid, "tm", split_axis=0, concat_axis=2, tiled=True)
    beam_local = intensity.shape[0]
    frame_count = intensity.shape[2] // UPCH
    frame_grid = intensity.reshape(beam_local, chan_count, frame_count, UPCH)
    centred = frame_grid - jnp.mean(frame_grid, axis=2, keepdims=True)
    frame_index = jnp.arange(frame_count)
    angles = (frame_index[:, None] * frame_index[None, :] % frame_count).astype(jnp.float32) * (
        TWO_PI / frame_count
    )
    forward = jnp.concatenate([jnp.cos(angles), -jnp.sin(angles)], axis=1)
    fine_local = chan_count * UPCH
    transformed = jnp.einsum("bcnk,nw->wbck", centred, forward, precision=HIGHEST)
    transformed = transformed.reshape(2, frame_count, beam_local, fine_local)
    trial_count = delays.shape[0]
    delay_cols = jnp.transpose(delays)
    bin_block = min(16, frame_count)

    def dedisperse(bin_start):
        frequency = bin_start + jnp.arange(bin_block)
        angle_grid = (frequency[:, None, None] * delay_cols[None, :, :] % frame_count).astype(
            jnp.float32
        ) * (TWO_PI / frame_count)
        cos_table = jnp.cos(angle_grid)
        sin_table = jnp.sin(angle_grid)
        table = jnp.concatenate(
            [
                jnp.concatenate([cos_table, -sin_table], axis=2),
                jnp.concatenate([sin_table, cos_table], axis=2),
            ],
            axis=1,
        )
        left_real = lax.dynamic_slice_in_dim(transformed[0], bin_start, bin_block, 0)
        left_imag = lax.dynamic_slice_in_dim(transformed[1], bin_start, bin_block, 0)
        left_side = jnp.concatenate([left_real, left_imag], axis=2)
        return jnp.einsum("vbk,vkd->vbd", left_side, table, precision=HIGHEST)

    trials = lax.map(dedisperse, jnp.arange(frame_count // bin_block) * bin_block)
    trials = trials.reshape(frame_count, beam_local, 2, trial_count)
    inverse = jnp.stack([jnp.cos(angles), -jnp.sin(angles)]) / (frame_count * math.sqrt(FINE))
    combined = lax.psum_scatter(trials, "channel", scatter_dimension=3, tiled=True)
    dedispersed = jnp.einsum("vbrd,rvn->bdn", combined, inverse, precision=HIGHEST)
    return (intensity, dedispersed)


def solution(mesh):
    return jax.shard_map(
        per_device,
        mesh=mesh,
        in_specs=(P(None, ("beam", "channel"), None, "tm"), P(), P(None, "channel")),
        out_specs=(P(("beam", "tm"), "channel", None), P(("beam", "tm"), "channel", None)),
        check_vma=False,
    )
```

profile of v0, /device:TPU:0, one launch (start us, length us, event | category | flops | bytes accessed | tf_op | source)
XLA Modules:
  0.0 1423.7 jit_solution(7562544665450734379)
XLA Ops:
  17.5 368.9 %all_to_all.36 = bf16[2,256,64,256]{3,1,0,2:T(8,128)(2,1)S(1)} all-to-all(bf16[2,256,64,256]{3,1,0,2:T(8,128)(2,1)S(1)} %copy.27), channel_id=1, replica_groups=mesh['channel'=4,'tm'=4,'beam'=2] {'channel'}, dimensions={2} | all-to-all | bytes 33554432 | tf_op jit(solution)/shard_map/all_to_all | solution.py:66
  386.4 11.2 copy.29
  398.4 19.3 %fusion.103 = bf16[512,2048]{1,0:T(8,128)(2,1)} fusion(s32[2048]{0:T(1024)S(1)} %get-tuple-element.115, s32[512]{0:T(512)S(1)} %get-tuple-element.127, s32[2048]{0:T(1024)S(1)} %get-tuple-element.114, s32[512]{0:T(512)S(1)} %get-tuple-element.128), kind=kLoop, calls=%fused_computation.179 | loop fusion | flops 37748736 | bytes 2117632 | tf_op jit(solution)/shard_map/neg | solution.py:44
  417.6 20.6 %multiply_convert_fusion = (bf16[512,2048]{1,0:T(8,128)(2,1)S(1)}, bf16[512,2048]{1,0:T(8,128)(2,1)}) fusion(s32[2048]{0:T(1024)S(1)} %get-tuple-element.115, s32[512]{0:T(512)S(1)} %get-tuple-element.127, s32[2048]{0:T(1024)S(1)} %get-tuple-element.114, s32[512]{0:T(512)S(1)} %get-tuple-element.128), kind=kLoop, calls=%fused_computation.85 | loop fusion | flops 36700160 | bytes 4214784 | tf_op jit(solution)/shard_map/convert_element_type | solution.py:43
  438.2 348.5 %all-gather.2.cloned.1.call-done = bf16[2,2048,16,256]{3,2,1,0:T(8,128)(2,1)} async-done(((bf16[2,1024,16,256]{3,2,1,0:T(8,128)(2,1)}), bf16[2,2048,16,256]{3,2,1,0:T(8,128)(2,1)}) %all-gather.2.cloned.1.call-update) | async-done | bytes 33554448 | tf_op jit(solution)/shard_map/all_gather | solution.py:71
  786.7 22.6 %copy.46 = bf16[512,8,16,256]{3,1,2,0:T(8,128)(2,1)} copy(bf16[512,8,16,256]{3,2,1,0:T(8,128)(2,1)} %bitcast.68) | data formatting | bytes 67108864
  809.3 44.5 %fusion.49 = bf16[1024,4096]{1,0:T(8,128)(2,1)} fusion(bf16[4096,4096]{1,0:T(8,128)(2,1)} %bitcast.69, bf16[512,2048]{1,0:T(8,128)(2,1)} %get-tuple-element.113, bf16[512,2048]{1,0:T(8,128)(2,1)S(1)} %get-tuple-element.112, bf16[512,2048]{1,0:T(8,128)(2,1)} %fusion.103), kind=kOutput, calls=%fused_computation.72 | convolution fusion | flops 34397487104 | bytes 48234496 | tf_op jit(solution)/shard_map/dot_general | solution.py:75
  891.9 62.1 %multiply_add_fusion = f32[2,512,16,256]{3,2,1,0:T(8,128)} fusion(bf16[2,512,16,256]{3,2,1,0:T(8,128)(2,1)} %bitcast.67, bf16[2,512,16,112]{3,2,1,0:T(8,128)(2,1)} %copy.31, f32[256]{0:T(256)S(1)} %mul.404, f32[256]{0:T(256)S(1)} %mul.401, f32[256]{0:T(256)S(1)} %mul.398, f32[256]{0:T(256)S(1)} %mul.395, f32[256]{0:T(256)S(1)} %mul.392, f32[256]{0:T(256)S(1)} %mul.389, ...), kind=kLoop, calls=%fused_computation.38 | loop fusion | flops 184549376 | bytes 28844032 | tf_op jit(solution)/shard_map/add | solution.py:86
  954.0 10.9 fusion.105
  965.0 10.8 squeeze.16
  982.9 10.8 squeeze.15
  1001.4 18.0 %fusion.28 = f32[8192,2,256]{2,0,1:T(8,128)} fusion(f32[8192,2,128]{2,0,1:T(8,128)S(1)} %copy-done, f32[8192,2,128]{2,0,1:T(8,128)} %copy.32, f32[128,128]{1,0:T(8,128)S(1)} %get-tuple-element.118, f32[128,128]{1,0:T(8,128)S(1)} %get-tuple-element.117, f32[128,128]{1,0:T(8,128)S(1)} %get-tuple-element.116), kind=kOutput, calls=%fused_computation.34 | convolution fusion | flops 12889292800 | bytes 33751040 | tf_op jit(solution)/shard_map/dot_general | solution.py:93
  1025.7 31.3 %copy.34 = f32[8192,2,128]{2,1,0:T(2,128)} copy(f32[8192,2,128]{2,0,1:T(8,128)S(1)} %fusion.38) | data formatting | bytes 16777216 | tf_op jit(solution)/shard_map/add | solution.py:96
  1057.0 11.5 reshape.221
  1068.5 39.4 %all-to-all-start.1 = ((f32[512,16,256]{2,1,0:T(8,128)}), f32[512,16,256]{2,1,0:T(8,128)}, u32[]{:S(2)}, u32[]{:S(2)}) async-start(f32[512,16,256]{2,1,0:T(8,128)} %reshape.221), calls=%async_computation.1 | async-start | bytes 16777216 | tf_op jit(solution)/shard_map/all_to_all | solution.py:99
  1108.0 93.0 %all-to-all-done.1 = f32[512,16,256]{2,1,0:T(8,128)} async-done(((f32[512,16,256]{2,1,0:T(8,128)}), f32[512,16,256]{2,1,0:T(8,128)}, u32[]{:S(2)}, u32[]{:S(2)}) %all-to-all-start.1) | async-done | bytes 8388640 | tf_op jit(solution)/shard_map/all_to_all | solution.py:99
  1234.8 16.1 %fusion.47 = f32[2,64,128,256]{3,1,2,0:T(8,128)S(1)} fusion(f32[2,64,64,1]{2,1,3,0:T(8,128)S(1)} %bitcast.74, f32[128,256,64]{1,2,0:T(8,128)} %copy.38), kind=kOutput, calls=%fused_computation.63 | convolution fusion | flops 3221225472 | bytes 25198592 | tf_op jit(solution)/shard_map/bcnk,nw->wbck/dot_general | solution.py:110
  1250.9 19.7 %copy.39 = f32[2,64,128,256]{3,2,1,0:T(8,128)} copy(f32[2,64,128,256]{3,1,2,0:T(8,128)S(1)} %fusion.47) | data formatting | bytes 33554432 | tf_op jit(solution)/shard_map/while | solution.py:135
  1270.6 96.8 %while.12 = (s32[]{:T(128)}, f32[4,16,128,64]{2,3,1,0:T(8,128)}, f32[2,64,128,256]{3,2,1,0:T(8,128)}, s32[4]{0:T(128)S(1)}, s32[256,32]{0,1:T(8,128)S(1)}, /*index=5*/s32[]{:T(128)}, s32[]{:T(128)}, s32[]{:T(128)}) while((s32[]{:T(128)}, f32[4,16,128,64]{2,3,1,0:T(8,128)}, f32[2,64,128,256]{3,2,1,0:T(8,128)}, s32[4]{0:T(128)S(1)}, ...), condition=%wide.region_3.4_spmd, body=%wide.region_2.3_spmd.sunk | while | flops 809893888 | bytes 49840404 | solution.py:135
  1273.9 11.0 fusion.118
  1298.1 11.0 fusion.118
  1322.3 11.0 fusion.118
  1346.5 11.0 fusion.118
  1380.6 33.9 %reduce-scatter.2.cloned.1.call-done = f32[64,128,2,8]{1,0,2,3:T(8,128)} async-done(((f32[64,128,2,32]{1,0,2,3:T(8,128)}), f32[64,128,2,8]{1,0,2,3:T(8,128)}) %reduce-scatter.2.cloned.1.call-update) | async-done | bytes 524304 | tf_op jit(solution)/shard_map/reduce_scatter | solution.py:138
  (77 shorter events, 164.8 us)
Async XLA Ops:
  7.2 779.5 %all-gather.2.cloned.1.call-start = ((), (), s32[]{:S(2)}) async-start(), calls=%async_computation.3 | async-start | bytes 50331648 | tf_op jit(solution)/shard_map/all_gather | solution.py:71
  397.7 0.7 copy-start.2
  876.2 7.9 collective-permute-start
  993.7 7.7 copy-start
  1068.5 132.6 %all-to-all-start.1 = ((f32[512,16,256]{2,1,0:T(8,128)}), f32[512,16,256]{2,1,0:T(8,128)}, u32[]{:S(2)}, u32[]{:S(2)}) async-start(f32[512,16,256]{2,1,0:T(8,128)} %reshape.221), calls=%async_computation.1 | async-start | bytes 16777216 | tf_op jit(solution)/shard_map/all_to_all | solution.py:99
  1107.8 306.6 %reduce-scatter.2.cloned.1.call-start = ((), (), s32[]{:S(2)}) async-start(), calls=%async_computation.4 | async-start | bytes 2621440 | tf_op jit(solution)/shard_map/reduce_scatter | solution.py:138
  1250.9 19.7 %copy-start.1 = (s32[32,256]{1,0:T(8,128)S(1)}, s32[32,256]{1,0:T(8,128)}, u32[]{:S(2)}) copy-start(s32[32,256]{1,0:T(8,128)} %param.7) | copy-start | bytes 98308
Sparse Core Ops, SparseCore 0:
  397.8 388.8 all-gather.1
  1371.7 42.6 reduce-scatter.1
where the time goes:
time: 1430 us; the launch traced here: 1420 us
  waiting for transfers between devices  477 us (33%)
  blocking collectives  369 us (26%)
  local copies, waits for them, and re-layouts  281 us (20%)
  other arithmetic  129 us (9%)
  matrix products  103 us (7%)
  starting transfers between devices  42.8 us (3%)
  between operations  15 us (1%)
    all_to_all x1, blocking collectives, per_device(): lax.all_to_all(voltages, 'channel', split_axis=2, concat_axis=1, tiled=True)  369 us
    all_gather x1, waiting for transfers between devices, per_device(): feed_piece = lax.all_gather(by_channel, 'beam', axis=1, tiled=True)  348 us
    all_to_all x1, waiting for transfers between devices, per_device(): lax.all_to_all(power_grid, 'tm', split_axis=0, concat_axis=2, tiled=True)  93 us
    add x1, other arithmetic, per_device(): filtered + extended[:, :, :, tap_index * UPCH:tap_index * UPCH + sample_c...  62.1 us
    unnamed x11, local copies, waits for them, and re-layouts  59.5 us
    dot_general x1, matrix products, per_device(): summed = jnp.dot(weights, flat_piece, preferred_element_type=jnp.float32)  44.5 us
    slice x4, local copies, waits for them, and re-layouts, dedisperse(): transformed[0]  43.9 us
    all_to_all x1, starting transfers between devices, per_device(): lax.all_to_all(power_grid, 'tm', split_axis=0, concat_axis=2, tiled=True)  39.4 us
  transfers between devices with their start and end apart: 4, of which 4 were waited for; matrix products, arithmetic and copies ran while one was open for 4% of the time, Pallas kernels for 0%

commit v1 on v0

--- a/solution.py
+++ b/solution.py
@@ -68,7 +68,10 @@
     sample_count = by_channel.shape[3]
     own_beams = BEAMS // lax.axis_size("beam")
     beam_start = lax.axis_index("beam") * own_beams
-    feed_piece = lax.all_gather(by_channel, "beam", axis=1, tiled=True)
+    peers = lax.axis_size("beam")
+    tiles = jnp.stack([by_channel for _ in range(peers)])
+    tiles = lax.all_to_all(tiles, "beam", split_axis=0, concat_axis=0)
+    feed_piece = jnp.concatenate(tiles, axis=1)
     piece_width = feed_piece.shape[1]
     weights = steering(positions, beam_start, own_beams, places, FEEDS)
     flat_piece = feed_piece.reshape(2 * piece_width, chan_count * sample_count)

time: 1430 us -> 1460 us (1.021)
  waiting for transfers between devices: 477 us -> 450 us
  other arithmetic: 129 us -> 151 us
  local copies, waits for them, and re-layouts: 281 us -> 303 us
    all_gather x1 -> x0, waiting for transfers between devices: 348 us -> none  [per_device(): feed_piece = lax.all_gather(by_channel, 'beam', axis=1, tiled=True)]
    all_to_all x0 -> x1, waiting for transfers between devices: none -> 321 us  [per_device(): tiles = lax.all_to_all(tiles, 'beam', split_axis=0, concat_axis=0)]
    reshape x0 -> x1, local copies, waits for them, and re-layouts: none -> 22.8 us  [per_device(): feed_piece = jnp.concatenate(tiles, axis=1)]
    another operation x0 -> x1, other arithmetic: none -> 22.4 us  [per_device(): tiles = jnp.stack([by_channel for _ in range(peers)])]
  transfers between devices with their start and end apart: 4 -> 4, of which waited for: 4 -> 4; matrix products, arithmetic and copies ran while one was open for 4% -> 3% of each run, Pallas kernels for 0% -> 0%
where the time goes in v1:
time: 1460 us; the launch traced here: 1450 us
  waiting for transfers between devices  450 us (31%)
  blocking collectives  369 us (25%)
  local copies, waits for them, and re-layouts  303 us (21%)
  other arithmetic  151 us (10%)
  matrix products  103 us (7%)
  starting transfers between devices  55.8 us (4%)
  between operations  15.1 us (1%)
    all_to_all x1, blocking collectives, per_device(): lax.all_to_all(voltages, 'channel', split_axis=2, concat_axis=1, tiled=True)  369 us
    all_to_all x1, waiting for transfers between devices, per_device(): tiles = lax.all_to_all(tiles, 'beam', split_axis=0, concat_axis=0)  321 us
    all_to_all x1, waiting for transfers between devices, per_device(): lax.all_to_all(power_grid, 'tm', split_axis=0, concat_axis=2, tiled=True)  93 us
    add x1, other arithmetic, per_device(): filtered + extended[:, :, :, tap_index * UPCH:tap_index * UPCH + sample_c...  62 us
    unnamed x11, local copies, waits for them, and re-layouts  58.8 us
    dot_general x1, matrix products, per_device(): summed = jnp.dot(weights, flat_piece, preferred_element_type=jnp.float32)  44.4 us
    slice x4, local copies, waits for them, and re-layouts, dedisperse(): transformed[0]  43.8 us
    all_to_all x1, starting transfers between devices, per_device(): lax.all_to_all(power_grid, 'tm', split_axis=0, concat_axis=2, tiled=True)  39.6 us
  transfers between devices with their start and end apart: 4, of which 4 were waited for; matrix products, arithmetic and copies ran while one was open for 3% of the time, Pallas kernels for 0%

profile of v1, /device:TPU:0, one launch (start us, length us, event | category | flops | bytes accessed | tf_op | source)
XLA Modules:
  0.0 1454.9 jit_solution(15545338272840736354)
XLA Ops:
  17.5 368.9 %all_to_all.38 = bf16[2,256,64,256]{3,1,0,2:T(8,128)(2,1)S(1)} all-to-all(bf16[2,256,64,256]{3,1,0,2:T(8,128)(2,1)S(1)} %copy.29), channel_id=1, replica_groups=mesh['channel'=4,'tm'=4,'beam'=2] {'channel'}, dimensions={2} | all-to-all | bytes 33554432 | tf_op jit(solution)/shard_map/all_to_all | solution.py:66
  386.4 11.2 copy.31
  397.6 22.4 %pad_maximum_fusion = bf16[2,2,1024,16,256]{4,3,2,1,0:T(8,128)(2,1)} fusion(bf16[1,2,1024,16,256]{4,3,2,1,0:T(8,128)(2,1)} %bitcast.66), kind=kLoop, calls=%fused_computation.28 | loop fusion | flops 16777216 | bytes 50331648 | tf_op jit(solution)/shard_map/stack | solution.py:72
  420.1 13.0 all-to-all-start.1
  433.1 19.3 %fusion.103 = bf16[512,2048]{1,0:T(8,128)(2,1)} fusion(s32[2048]{0:T(1024)S(1)} %get-tuple-element.115, s32[512]{0:T(512)S(1)} %get-tuple-element.127, s32[2048]{0:T(1024)S(1)} %get-tuple-element.114, s32[512]{0:T(512)S(1)} %get-tuple-element.128), kind=kLoop, calls=%fused_computation.180 | loop fusion | flops 37748736 | bytes 2117632 | tf_op jit(solution)/shard_map/neg | solution.py:44
  452.4 20.6 %multiply_convert_fusion = (bf16[512,2048]{1,0:T(8,128)(2,1)S(1)}, bf16[512,2048]{1,0:T(8,128)(2,1)}) fusion(s32[2048]{0:T(1024)S(1)} %get-tuple-element.115, s32[512]{0:T(512)S(1)} %get-tuple-element.127, s32[2048]{0:T(1024)S(1)} %get-tuple-element.114, s32[512]{0:T(512)S(1)} %get-tuple-element.128), kind=kLoop, calls=%fused_computation.86 | loop fusion | flops 36700160 | bytes 4214784 | tf_op jit(solution)/shard_map/convert_element_type | solution.py:43
  472.9 321.3 %all-to-all-done.1 = bf16[2,2,1024,16,256]{4,3,2,1,0:T(8,128)(2,1)} async-done(((bf16[2,2,1024,16,256]{4,3,2,1,0:T(8,128)(2,1)}), bf16[2,2,1024,16,256]{4,3,2,1,0:T(8,128)(2,1)}, u32[]{:S(2)}, u32[]{:S(2)}) %all-to-all-start.1) | async-done | bytes 33554464 | tf_op jit(solution)/shard_map/all_to_all | solution.py:73
  794.2 22.8 %copy.32 = bf16[2,2,1024,16,256]{4,3,2,1,0:T(8,128)(2,1)} copy(bf16[2,2,1024,16,256]{4,3,2,0,1:T(8,128)(2,1)} %bitcast.8) | data formatting | bytes 67108864 | tf_op jit(solution)/shard_map/reshape | solution.py:74
  817.1 22.6 %copy.49 = bf16[512,8,16,256]{3,1,2,0:T(8,128)(2,1)} copy(bf16[512,8,16,256]{3,2,1,0:T(8,128)(2,1)} %bitcast.62) | data formatting | bytes 67108864
  839.7 44.4 %fusion.49 = bf16[1024,4096]{1,0:T(8,128)(2,1)} fusion(bf16[4096,4096]{1,0:T(8,128)(2,1)} %bitcast.70, bf16[512,2048]{1,0:T(8,128)(2,1)} %get-tuple-element.113, bf16[512,2048]{1,0:T(8,128)(2,1)S(1)} %get-tuple-element.112, bf16[512,2048]{1,0:T(8,128)(2,1)} %fusion.103), kind=kOutput, calls=%fused_computation.73 | convolution fusion | flops 34397487104 | bytes 48234496 | tf_op jit(solution)/shard_map/dot_general | solution.py:78
  922.0 62.0 %multiply_add_fusion = f32[2,512,16,256]{3,2,1,0:T(8,128)} fusion(bf16[2,512,16,256]{3,2,1,0:T(8,128)(2,1)} %bitcast.69, bf16[2,512,16,112]{3,2,1,0:T(8,128)(2,1)} %copy.34, f32[256]{0:T(256)S(1)} %mul.404, f32[256]{0:T(256)S(1)} %mul.401, f32[256]{0:T(256)S(1)} %mul.398, f32[256]{0:T(256)S(1)} %mul.395, f32[256]{0:T(256)S(1)} %mul.392, f32[256]{0:T(256)S(1)} %mul.389, ...), kind=kLoop, calls=%fused_computation.39 | loop fusion | flops 184549376 | bytes 28844032 | tf_op jit(solution)/shard_map/add | solution.py:89
  1031.3 18.0 %fusion.28 = f32[8192,2,256]{2,0,1:T(8,128)} fusion(f32[8192,2,128]{2,0,1:T(8,128)S(1)} %copy-done, f32[8192,2,128]{2,0,1:T(8,128)} %copy.35, f32[128,128]{1,0:T(8,128)S(1)} %get-tuple-element.118, f32[128,128]{1,0:T(8,128)S(1)} %get-tuple-element.117, f32[128,128]{1,0:T(8,128)S(1)} %get-tuple-element.116), kind=kOutput, calls=%fused_computation.35 | convolution fusion | flops 12889292800 | bytes 33751040 | tf_op jit(solution)/shard_map/dot_general | solution.py:96
  1055.6 31.3 %copy.37 = f32[8192,2,128]{2,1,0:T(2,128)} copy(f32[8192,2,128]{2,0,1:T(8,128)S(1)} %fusion.38) | data formatting | bytes 16777216 | tf_op jit(solution)/shard_map/add | solution.py:99
  1086.8 11.5 reshape.222
  1098.3 39.6 %all-to-all-start.2 = ((f32[512,16,256]{2,1,0:T(8,128)}), f32[512,16,256]{2,1,0:T(8,128)}, u32[]{:S(2)}, u32[]{:S(2)}) async-start(f32[512,16,256]{2,1,0:T(8,128)} %reshape.222), calls=%async_computation.2 | async-start | bytes 16777216 | tf_op jit(solution)/shard_map/all_to_all | solution.py:102
  1138.2 93.0 %all-to-all-done.2 = f32[512,16,256]{2,1,0:T(8,128)} async-done(((f32[512,16,256]{2,1,0:T(8,128)}), f32[512,16,256]{2,1,0:T(8,128)}, u32[]{:S(2)}, u32[]{:S(2)}) %all-to-all-start.2) | async-done | bytes 8388640 | tf_op jit(solution)/shard_map/all_to_all | solution.py:102
  1264.8 16.1 %fusion.47 = f32[2,64,128,256]{3,1,2,0:T(8,128)S(1)} fusion(f32[2,64,64,1]{2,1,3,0:T(8,128)S(1)} %bitcast.75, f32[128,256,64]{1,2,0:T(8,128)} %copy.41), kind=kOutput, calls=%fused_computation.64 | convolution fusion | flops 3221225472 | bytes 25198592 | tf_op jit(solution)/shard_map/bcnk,nw->wbck/dot_general | solution.py:113
  1280.9 19.7 %copy.42 = f32[2,64,128,256]{3,2,1,0:T(8,128)} copy(f32[2,64,128,256]{3,1,2,0:T(8,128)S(1)} %fusion.47) | data formatting | bytes 33554432 | tf_op jit(solution)/shard_map/while | solution.py:138
  1300.6 98.0 %while.12 = (s32[]{:T(128)}, f32[4,16,128,64]{2,3,1,0:T(8,128)}, f32[2,64,128,256]{3,2,1,0:T(8,128)}, s32[4]{0:T(128)S(1)}, s32[256,32]{0,1:T(8,128)S(1)}, /*index=5*/s32[]{:T(128)}, s32[]{:T(128)}, s32[]{:T(128)}) while((s32[]{:T(128)}, f32[4,16,128,64]{2,3,1,0:T(8,128)}, f32[2,64,128,256]{3,2,1,0:T(8,128)}, s32[4]{0:T(128)S(1)}, ...), condition=%wide.region_3.4_spmd, body=%wide.region_2.3_spmd.sunk | while | flops 809893888 | bytes 49840404 | solution.py:138
  1304.0 11.0 fusion.118
  1328.5 11.0 fusion.118
  1353.0 11.0 fusion.118
  1377.5 11.0 fusion.118
  1411.8 33.9 %reduce-scatter.2.cloned.1.call-done = f32[64,128,2,8]{1,0,2,3:T(8,128)} async-done(((f32[64,128,2,32]{1,0,2,3:T(8,128)}), f32[64,128,2,8]{1,0,2,3:T(8,128)}) %reduce-scatter.2.cloned.1.call-update) | async-done | bytes 524304 | tf_op jit(solution)/shard_map/reduce_scatter | solution.py:141
  (78 shorter events, 196.6 us)
Async XLA Ops:
  420.0 13.0 copy-start.2
  420.1 374.2 %all-to-all-start.1 = ((bf16[2,2,1024,16,256]{4,3,2,1,0:T(8,128)(2,1)}), bf16[2,2,1024,16,256]{4,3,2,1,0:T(8,128)(2,1)}, u32[]{:S(2)}, u32[]{:S(2)}) async-start(bf16[2,2,1024,16,256]{4,3,2,1,0:T(8,128)(2,1)} %pad_maximum_fusion), calls=%async_computation.1 | async-start | bytes 67108864 | tf_op jit(solution)/shard_map/all_to_all | solution.py:73
  906.6 7.6 collective-permute-start
  1023.6 7.7 copy-start
  1098.3 132.8 %all-to-all-start.2 = ((f32[512,16,256]{2,1,0:T(8,128)}), f32[512,16,256]{2,1,0:T(8,128)}, u32[]{:S(2)}, u32[]{:S(2)}) async-start(f32[512,16,256]{2,1,0:T(8,128)} %reshape.222), calls=%async_computation.2 | async-start | bytes 16777216 | tf_op jit(solution)/shard_map/all_to_all | solution.py:102
  1138.0 307.7 %reduce-scatter.2.cloned.1.call-start = ((), (), s32[]{:S(2)}) async-start(), calls=%async_computation.4 | async-start | bytes 2621440 | tf_op jit(solution)/shard_map/reduce_scatter | solution.py:141
  1280.9 19.7 %copy-start.1 = (s32[32,256]{1,0:T(8,128)S(1)}, s32[32,256]{1,0:T(8,128)}, u32[]{:S(2)}) copy-start(s32[32,256]{1,0:T(8,128)} %param.7) | copy-start | bytes 98308
Sparse Core Ops, SparseCore 0:
  1402.9 42.6 reduce-scatter.1
